TPU v7x, 32 devices: a whole 2x2x4 slice. The times are simulated.
32 devices in a mesh: dp: 4 (over x, core), seq: 2 (over y), tensor: 4 (over z).
Axes of the slice: x: 2, y: 2, z: 4, core: 2. Of those that a mesh axis runs over, the one named last changes fastest.
Arguments:
- tokens: bfloat16 [2048, 4096], P(('dp', 'seq')), may hold values from -6 to 6
- seg_ids: int32 [2048], P('dp'), may hold values from 0 to 15, as said below
- gain_attn: bfloat16 [4096], P(('dp', 'seq')), may hold values from 0.5 to 1.5
- w_query: bfloat16 [4096, 4096], P(('dp', 'seq'), 'tensor'), may hold values from -1.5 to 1.5
- kv_weight: bfloat16 [4096, 512], P(('dp', 'seq')), may hold values from -1.5 to 1.5
- w_out: bfloat16 [4096, 4096], P('tensor', ('dp', 'seq')), may hold values from -0.375 to 0.375
- gain_ffn: bfloat16 [4096], P(('dp', 'seq')), may hold values from 0.5 to 1.5
- w_gate: bfloat16 [4096, 12288], P(('dp', 'seq'), 'tensor'), may hold values from -0.09375 to 0.09375
- w_up: bfloat16 [4096, 12288], P(('dp', 'seq'), 'tensor'), may hold values from -0.09375 to 0.09375
- w_down: bfloat16 [12288, 4096], P('tensor', ('dp', 'seq')), may hold values from -0.0546875 to 0.0546875
- d_out: bfloat16 [2048, 4096], P(('dp', 'seq')), may hold values from -6 to 6
Outputs:
- out: bfloat16 [2048, 4096], P(('dp', 'seq'))
- d_tokens: float32 [2048, 4096], P(('dp', 'seq'))
- d_gain_attn: float32 [4096], P(('dp', 'seq'))
- d_w_query: float32 [4096, 4096], P(('dp', 'seq'), 'tensor')
- d_kv_weight: float32 [4096, 512], P(('dp', 'seq'))
- d_w_out: float32 [4096, 4096], P('tensor', ('dp', 'seq'))
- d_gain_ffn: float32 [4096], P(('dp', 'seq'))
- d_w_gate: float32 [4096, 12288], P(('dp', 'seq'), 'tensor')
- d_w_up: float32 [4096, 12288], P(('dp', 'seq'), 'tensor')
- d_w_down: float32 [12288, 4096], P('tensor', ('dp', 'seq'))
Inputs may be any that keep to these rules, and one draw needn't show every extreme that they name: `seg_ids`: within each group of 512 tokens g (from 0) the ids never fall, take values from 4 g to 4 g + 3 and start at 4 g; some group other than the last holds one sequence.
All inputs are finite; a program needn't handle non-finite values.
Results may differ from a plain program's by a relative error of at most 0.02.
Values may be sent and summed in bfloat16 or wider, within the bound.
A program may use at most 384 MiB of HBM per device.

v0:
```python
import math
import jax
import jax.numpy as jnp
from jax import lax
from jax.sharding import PartitionSpec as P

HD = 256
EPS = 1e-06
NEG = -1e30


def place_tables(segs):
    length = segs.shape[0]
    index = jnp.arange(length, dtype=jnp.int32)
    flags = jnp.concatenate([jnp.ones((1,), dtype=bool), segs[1:] != segs[:-1]])
    starts = lax.cummax(jnp.where(flags, index, jnp.zeros_like(index)), axis=0)
    places = index - starts
    half_size = HD // 2
    freqs = jnp.exp(jnp.arange(half_size, dtype=jnp.float32) * (-math.log(10000.0) / half_size))
    angles = places.astype(jnp.float32)[:, None] * freqs[None, :]
    return (places, jnp.cos(angles), jnp.sin(angles))


def rotate(vector, cos_table, sin_table):
    half_size = vector.shape[-1] // 2
    leading = vector[..., :half_size]
    trailing = vector[..., half_size:]
    return jnp.concatenate(
        [leading * cos_table - trailing * sin_table, trailing * cos_table + leading * sin_table],
        axis=-1,
    )


def rotate_back(vector, cos_table, sin_table):
    half_size = vector.shape[-1] // 2
    leading = vector[..., :half_size]
    trailing = vector[..., half_size:]
    return jnp.concatenate(
        [leading * cos_table + trailing * sin_table, trailing * cos_table - leading * sin_table],
        axis=-1,
    )


def matmul(left, right):
    return jnp.dot(left, right, preferred_element_type=jnp.float32)


def matmul_nt(left, right):
    return lax.dot_general(
        left, right, (((1,), (1,)), ((), ())), preferred_element_type=jnp.float32
    )


def matmul_tn(left, right):
    return lax.dot_general(
        left, right, (((0,), (0,)), ((), ())), preferred_element_type=jnp.float32
    )


def gelu_tanh(values):
    return jax.nn.gelu(values, approximate=True)


def norm_back(d_act, normed, rms_val, gain_val):
    scaled = d_act * gain_val
    return rms_val * (scaled - normed * jnp.mean(scaled * normed, axis=-1, keepdims=True))


def shards(
    tokens, seg_ids, gain_attn, w_query, kv_weight, w_out, gain_ffn, w_gate, w_up, w_down, d_out
):
    rows = tokens.shape[0]
    scale_factor = 1.0 / math.sqrt(HD)
    offset = lax.axis_index("seq") * rows
    places, cos_table, sin_table = place_tables(seg_ids)
    own_places = lax.dynamic_slice_in_dim(places, offset, rows, 0)
    own_segs = lax.dynamic_slice_in_dim(seg_ids, offset, rows, 0)
    own_cos = lax.dynamic_slice_in_dim(cos_table, offset, rows, 0)
    own_sin = lax.dynamic_slice_in_dim(sin_table, offset, rows, 0)
    allowed = (own_segs[:, None] == seg_ids[None, :]) & (own_places[:, None] >= places[None, :])
    full_query, full_out, full_kv, full_gain_one = (
        lax.all_gather(w_query, ("dp", "seq"), axis=0, tiled=True),
        lax.all_gather(w_out, ("dp", "seq"), axis=1, tiled=True),
        lax.all_gather(kv_weight, ("dp", "seq"), axis=0, tiled=True),
        lax.all_gather(gain_attn, ("dp", "seq"), axis=0, tiled=True),
    )
    gain_one = full_gain_one.astype(jnp.float32)
    inputs = tokens.astype(jnp.float32)
    rms_one = lax.rsqrt(jnp.mean(inputs * inputs, axis=-1, keepdims=True) + EPS)
    norm_one = inputs * rms_one
    act_one = (norm_one * gain_one).astype(jnp.bfloat16)
    query_pre = matmul(act_one, full_query)
    heads = query_pre.shape[1] // HD
    kv_pre = matmul(act_one, full_kv)
    queries = (
        rotate(query_pre.reshape(rows, heads, HD), own_cos[:, None, :], own_sin[:, None, :])
        * scale_factor
    ).astype(jnp.bfloat16)
    own_kv = jnp.concatenate(
        [rotate(kv_pre[:, :HD], own_cos, own_sin), kv_pre[:, HD:]], axis=1
    ).astype(jnp.bfloat16)
    all_kv = lax.all_gather(own_kv, "seq", axis=0, tiled=True)
    keys = all_kv[:, :HD]
    values_all = all_kv[:, HD:]
    scores = jnp.einsum("rhd,kd->hrk", queries, keys, preferred_element_type=jnp.float32)
    scores = jnp.where(allowed[None], scores, NEG)
    top_score = jnp.max(scores, axis=-1, keepdims=True)
    expd = jnp.exp(scores - top_score)
    total = jnp.sum(expd, axis=-1, keepdims=True)
    log_total = top_score + jnp.log(total)
    probs_low = (expd / total).astype(jnp.bfloat16)
    mixed = (
        jnp.einsum("hrk,kd->rhd", probs_low, values_all, preferred_element_type=jnp.float32)
        .reshape(rows, heads * HD)
        .astype(jnp.bfloat16)
    )
    attn = lax.psum(matmul(mixed, full_out), "tensor")
    resid = inputs + attn
    full_gate, full_up, full_down, full_gain_two = (
        lax.all_gather(w_gate, ("dp", "seq"), axis=0, tiled=True),
        lax.all_gather(w_up, ("dp", "seq"), axis=0, tiled=True),
        lax.all_gather(w_down, ("dp", "seq"), axis=1, tiled=True),
        lax.all_gather(gain_ffn, ("dp", "seq"), axis=0, tiled=True),
    )
    gain_two = full_gain_two.astype(jnp.float32)
    rms_two = lax.rsqrt(jnp.mean(resid * resid, axis=-1, keepdims=True) + EPS)
    norm_two = resid * rms_two
    act_two = (norm_two * gain_two).astype(jnp.bfloat16)
    gate = matmul(act_two, full_gate)
    up_val = matmul(act_two, full_up)
    gelu_val, gelu_pull = jax.vjp(gelu_tanh, gate)
    hidden = (gelu_val * up_val).astype(jnp.bfloat16)
    ffn = lax.psum(matmul(hidden, full_down).astype(jnp.bfloat16), "tensor").astype(jnp.float32)
    out = (resid + ffn).astype(jnp.bfloat16)
    back_gate, back_up, back_down = (
        lax.all_gather(w_gate, ("dp", "seq"), axis=0, tiled=True),
        lax.all_gather(w_up, ("dp", "seq"), axis=0, tiled=True),
        lax.all_gather(w_down, ("dp", "seq"), axis=1, tiled=True),
    )
    d_hidden = matmul_nt(d_out, back_down)
    grad_down = matmul_tn(hidden, d_out)
    d_gate = gelu_pull(d_hidden * up_val)[0].astype(jnp.bfloat16)
    d_up = (d_hidden * gelu_val).astype(jnp.bfloat16)
    grad_gate = matmul_tn(act_two, d_gate)
    grad_up = matmul_tn(act_two, d_up)
    d_act_two = lax.psum(matmul_nt(d_gate, back_gate) + matmul_nt(d_up, back_up), "tensor")
    grad_gain_two = jnp.sum(d_act_two * norm_two, axis=0)
    d_resid = d_out.astype(jnp.float32) + norm_back(d_act_two, norm_two, rms_two, gain_two)
    ffn_grads = (
        lax.psum_scatter(
            grad_gate.astype(jnp.bfloat16), ("dp", "seq"), scatter_dimension=0, tiled=True
        ).astype(jnp.float32),
        lax.psum_scatter(
            grad_up.astype(jnp.bfloat16), ("dp", "seq"), scatter_dimension=0, tiled=True
        ).astype(jnp.float32),
        lax.psum_scatter(
            grad_down.astype(jnp.bfloat16), ("dp", "seq"), scatter_dimension=1, tiled=True
        ).astype(jnp.float32),
        lax.psum_scatter(
            grad_gain_two.astype(jnp.bfloat16), ("dp", "seq"), scatter_dimension=0, tiled=True
        ).astype(jnp.float32),
    )
    back_query, back_out, back_kv = (
        lax.all_gather(w_query, ("dp", "seq"), axis=0, tiled=True),
        lax.all_gather(w_out, ("dp", "seq"), axis=1, tiled=True),
        lax.all_gather(kv_weight, ("dp", "seq"), axis=0, tiled=True),
    )
    d_attn = d_resid.astype(jnp.bfloat16)
    grad_out = matmul_tn(mixed, d_attn)
    d_mixed = matmul_nt(d_attn, back_out).astype(jnp.bfloat16).reshape(rows, heads, HD)
    scores_again = jnp.einsum("rhd,kd->hrk", queries, keys, preferred_element_type=jnp.float32)
    probs = jnp.where(allowed[None], jnp.exp(scores_again - log_total), 0.0)
    d_probs = jnp.einsum("rhd,kd->hrk", d_mixed, values_all, preferred_element_type=jnp.float32)
    delta = jnp.sum(probs * d_probs, axis=-1, keepdims=True)
    d_scores = (probs * (d_probs - delta)).astype(jnp.bfloat16)
    d_queries = (
        jnp.einsum("hrk,kd->rhd", d_scores, keys, preferred_element_type=jnp.float32) * scale_factor
    )
    d_query_pre = (
        rotate_back(d_queries, own_cos[:, None, :], own_sin[:, None, :])
        .reshape(rows, heads * HD)
        .astype(jnp.bfloat16)
    )
    d_keys_part = jnp.einsum("hrk,rhd->kd", d_scores, queries, preferred_element_type=jnp.float32)
    d_values_part = jnp.einsum(
        "hrk,rhd->kd", probs.astype(jnp.bfloat16), d_mixed, preferred_element_type=jnp.float32
    )
    own_kv_grad = lax.psum_scatter(
        jnp.concatenate([d_keys_part, d_values_part], axis=1).astype(jnp.bfloat16),
        "seq",
        scatter_dimension=0,
        tiled=True,
    )
    d_act_query = matmul_nt(d_query_pre, back_query)
    d_act_sum, kv_grad = (
        lax.psum(d_act_query.astype(jnp.bfloat16), "tensor").astype(jnp.float32),
        lax.psum(own_kv_grad, "tensor").astype(jnp.float32),
    )
    d_kv_pre = jnp.concatenate(
        [rotate_back(kv_grad[:, :HD], own_cos, own_sin), kv_grad[:, HD:]], axis=1
    ).astype(jnp.bfloat16)
    d_act_one = d_act_sum + matmul_nt(d_kv_pre, back_kv)
    grad_query = matmul_tn(act_one, d_query_pre)
    grad_kv = matmul_tn(act_one, d_kv_pre)
    grad_gain_one = jnp.sum(d_act_one * norm_one, axis=0)
    d_tokens = d_resid + norm_back(d_act_one, norm_one, rms_one, gain_one)
    attn_grads = (
        lax.psum_scatter(
            grad_query.astype(jnp.bfloat16), ("dp", "seq"), scatter_dimension=0, tiled=True
        ).astype(jnp.float32),
        lax.psum_scatter(
            grad_out.astype(jnp.bfloat16), ("dp", "seq"), scatter_dimension=1, tiled=True
        ).astype(jnp.float32),
        lax.psum_scatter(
            grad_kv.astype(jnp.bfloat16), ("dp", "seq"), scatter_dimension=0, tiled=True
        ).astype(jnp.float32),
        lax.psum_scatter(
            grad_gain_one.astype(jnp.bfloat16), ("dp", "seq"), scatter_dimension=0, tiled=True
        ).astype(jnp.float32),
    )
    return (
        out,
        d_tokens,
        attn_grads[3],
        attn_grads[0],
        attn_grads[2],
        attn_grads[1],
        ffn_grads[3],
        ffn_grads[0],
        ffn_grads[1],
        ffn_grads[2],
    )


def solution(mesh):
    in_specs = (
        P(("dp", "seq"), None),
        P("dp"),
        P(("dp", "seq")),
        P(("dp", "seq"), "tensor"),
        P(("dp", "seq"), None),
        P("tensor", ("dp", "seq")),
        P(("dp", "seq")),
        P(("dp", "seq"), "tensor"),
        P(("dp", "seq"), "tensor"),
        P("tensor", ("dp", "seq")),
        P(("dp", "seq"), None),
    )
    out_specs = (
        P(("dp", "seq"), None),
        P(("dp", "seq"), None),
        P(("dp", "seq")),
        P(("dp", "seq"), "tensor"),
        P(("dp", "seq"), None),
        P("tensor", ("dp", "seq")),
        P(("dp", "seq")),
        P(("dp", "seq"), "tensor"),
        P(("dp", "seq"), "tensor"),
        P("tensor", ("dp", "seq")),
    )
    return jax.shard_map(shards, mesh=mesh, in_specs=in_specs, out_specs=out_specs, check_vma=False)
```

profile of v0, /device:TPU:0, one launch (start us, length us, event | category | flops | bytes accessed | tf_op | source)
XLA Modules:
  0.0 1815.9 jit_solution(10553113912535316646)
XLA Ops:
  10.2 0.8 slice_compare_fusion
  12.5 18.0 all-gather
  31.5 17.9 all-gather.9.cloned.1.call-done
  49.4 3.5 fusion.48
  53.7 10.2 all_gather.35
  63.8 42.2 %all-gather.11.cloned.1.call-done = bf16[4096,1024]{1,0:T(8,128)(2,1)} async-done(((bf16[512,1024]{1,0:T(8,128)(2,1)}), bf16[4096,1024]{1,0:T(8,128)(2,1)}) %all-gather.11.cloned.1.call-update) | async-done | bytes 8388624 | tf_op jit(solution)/shard_map/all_gather | solution.py:82
  106.1 6.8 fusion.46
  113.0 1.0 pad_maximum_fusion
  114.1 1.7 copy.57
  115.8 1.5 fusion.23
  117.7 0.9 copy-done.4
  119.2 1.5 convolution_convert_fusion.9
  120.8 43.1 %all-gather.13.cloned.1.call-done = bf16[1024,4096]{1,0:T(8,128)(2,1)} async-done(((bf16[1024,512]{1,0:T(8,128)(2,1)}), bf16[1024,4096]{1,0:T(8,128)(2,1)}) %all-gather.13.cloned.1.call-update) | async-done | bytes 8388624 | tf_op jit(solution)/shard_map/all_gather | solution.py:83
  163.8 8.0 fusion.51
  173.8 16.6 all-gather.1
  190.5 136.5 %all-reduce.8.cloned.1.call-done = f32[256,4096]{1,0:T(8,128)} async-done(((f32[256,4096]{1,0:T(8,128)}), f32[256,4096]{1,0:T(8,128)}) %all-reduce.8.cloned.1.call-update) | async-done | bytes 4194320 | tf_op jit(solution)/shard_map/psum | solution.py:117
  327.0 2.8 multiply_reduce_fusion.2
  329.8 2.0 copy-done
  331.8 1.9 multiply_convert_fusion
  333.7 119.2 %all-gather.17.cloned.1.call-done = bf16[4096,3072]{1,0:T(8,128)(2,1)} async-done(((bf16[512,3072]{1,0:T(8,128)(2,1)}), bf16[4096,3072]{1,0:T(8,128)(2,1)}) %all-gather.17.cloned.1.call-update) | async-done | bytes 25165840 | tf_op jit(solution)/shard_map/all_gather | solution.py:121
  452.9 13.7 fusion.53
  466.6 113.3 %all-gather.15.cloned.1.call-done = bf16[4096,3072]{1,0:T(8,128)(2,1)} async-done(((bf16[512,3072]{1,0:T(8,128)(2,1)}), bf16[4096,3072]{1,0:T(8,128)(2,1)}) %all-gather.15.cloned.1.call-update) | async-done | bytes 25165840 | tf_op jit(solution)/shard_map/all_gather | solution.py:120
  579.8 13.6 fusion.52
  593.4 118.5 %all-gather.19.cloned.1.call-done = bf16[3072,4096]{1,0:T(8,128)(2,1)} async-done(((bf16[3072,512]{1,0:T(8,128)(2,1)}), bf16[3072,4096]{1,0:T(8,128)(2,1)}) %all-gather.19.cloned.1.call-update) | async-done | bytes 25165840 | tf_op jit(solution)/shard_map/all_gather | solution.py:122
  711.9 17.4 multiply_convert_fusion.1
  729.3 13.4 fusion.54
  742.7 14.7 convolution_add_fusion.1
  757.5 1.3 log_add_fusion
  758.8 13.8 convolution_convert_fusion.7
  772.6 140.0 %all-reduce.10.cloned.1.call-done = f32[256,4096]{1,0:T(8,128)} async-done(((f32[256,4096]{1,0:T(8,128)}), f32[256,4096]{1,0:T(8,128)}) %all-reduce.10.cloned.1.call-update) | async-done | bytes 4194320 | tf_op jit(solution)/shard_map/psum | solution.py:146
  912.6 5.4 multiply_reduce_fusion
  918.5 3.1 multiply_add_fusion
  921.6 2.0 copy-done.3
  923.7 6.5 convolution_convert_fusion.8
  930.2 2.0 copy.83
  932.2 2.3 fusion.28
  937.0 0.8 pad_maximum_fusion.2
  938.1 1.0 add_convert_fusion.1
  939.2 7.1 convolution_convert_fusion.6
  946.3 5.3 reduce-scatter.8.cloned.1.call-done
  951.7 166.4 %all-reduce.12.cloned.1.call-done = (bf16[256,4096]{1,0:T(8,128)(2,1)}, bf16[256,4096]{1,0:T(8,128)(2,1)}, bf16[256,512]{1,0:T(8,128)(2,1)}) async-done(((bf16[256,4096]{1,0:T(8,128)(2,1)}, bf16[256,4096]{1,0:T(8,128)(2,1)}, bf16[256,512]{1,0:T(8,128)(2,1)}), (bf16[256,4096]{1,0:T(8,128)(2,1)}, bf16[256,4096]{1,0:T(8,128)(2,1)}, bf16[256,512]{1,0:T(8,128)(2,1)})) %all-reduce.12.cloned.1.call-update) | async-done | bytes 4456464 | tf_op jit(solution)/shard_map/psum | solution.py:133
  1118.1 0.9 slice.84
  1119.0 1.0 convert_element_type.159
  1120.8 3.5 convolution_convert_fusion.5
  1124.3 1.0 copy-done.9
  1125.3 8.3 convolution_convert_fusion.3
  1133.7 5.8 convolution_convert_fusion.4
  1140.0 13.7 convolution_convert_fusion
  1153.7 13.9 convolution_convert_fusion.1
  1167.7 13.5 convolution_convert_fusion.2
  1183.1 7.2 fusion.9
  1190.3 25.7 %all-reduce.2 = (bf16[4096]{0:T(1024)(128)(2,1)S(1)}, bf16[4096]{0:T(1024)(128)(2,1)S(1)}) all-reduce(bf16[4096]{0:T(1024)(128)(2,1)S(1)} %get-tuple-element.12, bf16[4096]{0:T(1024)(128)(2,1)S(1)} %copy-done.22), channel_id=3, replica_groups=mesh['dp'=4,'seq'=2,'tensor'=4] {'dp','seq'}, use_global_device_ids=true, to_apply=%region_16.17.clone | all-reduce | flops 8192 | bytes 32768
  1216.6 10.6 fusion.8
  1227.2 2.1 convert_element_type.165
  1229.4 20.3 %reduce-scatter.14.cloned.1.call-done = bf16[1024,512]{1,0:T(8,128)(2,1)} async-done(((bf16[1024,4096]{1,0:T(8,128)(2,1)}), bf16[1024,512]{1,0:T(8,128)(2,1)}) %reduce-scatter.14.cloned.1.call-update) | async-done | bytes 1048592 | tf_op jit(solution)/shard_map/reduce_scatter | solution.py:211
  1249.7 2.8 convert_element_type.167
  1252.5 72.2 %reduce-scatter.10.cloned.1.call-done = bf16[512,1024]{1,0:T(8,128)(2,1)} async-done(((bf16[4096,1024]{1,0:T(8,128)(2,1)}), bf16[512,1024]{1,0:T(8,128)(2,1)}) %reduce-scatter.10.cloned.1.call-update) | async-done | bytes 1048592 | tf_op jit(solution)/shard_map/reduce_scatter | solution.py:208
  1324.7 2.8 convert_element_type.163
  1327.4 156.7 %reduce-scatter.20.cloned.1.call-done = bf16[3072,512]{1,0:T(8,128)(2,1)} async-done(((bf16[3072,4096]{1,0:T(8,128)(2,1)}), bf16[3072,512]{1,0:T(8,128)(2,1)}) %reduce-scatter.20.cloned.1.call-update) | async-done | bytes 3145744 | tf_op jit(solution)/shard_map/reduce_scatter | solution.py:156
  1484.2 5.5 convert_element_type.175
  1489.7 154.3 %reduce-scatter.18.cloned.1.call-done = bf16[512,3072]{1,0:T(8,128)(2,1)} async-done(((bf16[4096,3072]{1,0:T(8,128)(2,1)}), bf16[512,3072]{1,0:T(8,128)(2,1)}) %reduce-scatter.18.cloned.1.call-update) | async-done | bytes 3145744 | tf_op jit(solution)/shard_map/reduce_scatter | solution.py:153
  1644.0 5.4 convert_element_type.173
  1649.4 154.4 %reduce-scatter.16.cloned.1.call-done = bf16[512,3072]{1,0:T(8,128)(2,1)} async-done(((bf16[4096,3072]{1,0:T(8,128)(2,1)}), bf16[512,3072]{1,0:T(8,128)(2,1)}) %reduce-scatter.16.cloned.1.call-update) | async-done | bytes 3145744 | tf_op jit(solution)/shard_map/reduce_scatter | solution.py:150
  1803.8 5.4 convert_element_type.171
  (127 shorter events, 15.8 us)
Async XLA Ops:
  7.2 23.9 %copy-start.23 = (s32[512]{0:T(512)S(1)}, s32[512]{0:T(512)}, u32[]{:S(2)}) copy-start(s32[512]{0:T(512)} %param.12) | copy-start | bytes 6148
  7.2 23.4 %copy-start.2 = (bf16[256,4096]{1,0:T(8,128)(2,1)S(1)}, bf16[256,4096]{1,0:T(8,128)(2,1)}, u32[]{:S(2)}) copy-start(bf16[256,4096]{1,0:T(8,128)(2,1)} %param.11) | copy-start | bytes 6291460
  7.2 42.2 %all-gather.9.cloned.1.call-start = ((), (), s32[]{:S(2)}) async-start(), calls=%async_computation.7 | async-start | bytes 4718592 | tf_op jit(solution)/shard_map/all_gather | solution.py:84
  7.9 98.1 %all-gather.11.cloned.1.call-start = ((), (), s32[]{:S(2)}) async-start(), calls=%async_computation.8 | async-start | bytes 9437184 | tf_op jit(solution)/shard_map/all_gather | solution.py:82
  8.7 155.2 %all-gather.13.cloned.1.call-start = ((), (), s32[]{:S(2)}) async-start(), calls=%async_computation.9 | async-start | bytes 9437184 | tf_op jit(solution)/shard_map/all_gather | solution.py:83
  9.4 317.5 %all-reduce.8.cloned.1.call-start = ((), (), s32[]{:S(2)}) async-start(), calls=%async_computation.10 | async-start | bytes 8388608 | tf_op jit(solution)/shard_map/psum | solution.py:117
  30.5 75.5 %copy-start.14 = (f32[8,1,512]{2,1,0:T(1,128)}, f32[8,1,512]{2,1,0:T(1,128)S(1)}, u32[]{:S(2)}) copy-start(f32[8,1,512]{2,1,0:T(1,128)S(1)} %convert_element_type.176) | copy-start | bytes 49156
  31.1 21.7 %copy-start.27 = (f32[256]{0:T(256)}, f32[256]{0:T(256)S(1)}, u32[]{:S(2)}) copy-start(f32[256]{0:T(256)S(1)} %add_rsqrt_fusion.1) | copy-start | bytes 3076
  53.5 59.4 %copy-start.11 = (f32[256,128]{0,1:T(8,128)}, f32[256,128]{0,1:T(8,128)S(1)}, u32[]{:S(2)}) copy-start(f32[256,128]{0,1:T(8,128)S(1)} %copy.54) | copy-start | bytes 393220
  53.6 59.3 %copy-start.13 = (f32[256,128]{0,1:T(8,128)}, f32[256,128]{0,1:T(8,128)S(1)}, u32[]{:S(2)}) copy-start(f32[256,128]{0,1:T(8,128)S(1)} %copy.56) | copy-start | bytes 393220
  115.8 3.5 copy-start.7
  117.3 1.3 copy-start.4
  117.3 1.3 copy-start.20
  118.6 0.6 copy-start.24
  171.8 281.1 %all-gather.17.cloned.1.call-start = ((), (), s32[]{:S(2)}) async-start(), calls=%async_computation.12 | async-start | bytes 28311552 | tf_op jit(solution)/shard_map/all_gather | solution.py:121
  172.4 1.4 copy-start.29
  172.4 407.4 %all-gather.15.cloned.1.call-start = ((), (), s32[]{:S(2)}) async-start(), calls=%async_computation.11 | async-start | bytes 28311552 | tf_op jit(solution)/shard_map/all_gather | solution.py:120
  173.0 538.9 %all-gather.19.cloned.1.call-start = ((), (), s32[]{:S(2)}) async-start(), calls=%async_computation.13 | async-start | bytes 28311552 | tf_op jit(solution)/shard_map/all_gather | solution.py:122
  173.8 738.8 %all-reduce.10.cloned.1.call-start = ((), (), s32[]{:S(2)}) async-start(), calls=%async_computation.14 | async-start | bytes 8388608 | tf_op jit(solution)/shard_map/psum | solution.py:146
  329.8 2.0 copy-start
  329.8 2.0 copy-start.25
  757.4 194.2 %reduce-scatter.8.cloned.1.call-start = ((), (), s32[]{:S(2)}) async-start(), calls=%async_computation.15 | async-start | bytes 786432 | tf_op jit(solution)/shard_map/reduce_scatter | solution.py:188
  912.6 5.4 copy-start.1
  912.6 5.9 copy-start.6
  912.6 5.9 copy-start.26
  921.6 2.0 copy-start.3
  923.6 8.6 copy-start.21
  932.2 2.4 copy-start.5
  932.2 2.5 copy-start.8
  932.2 2.6 copy-start.10
  936.0 2.1 copy-start.12
  937.8 180.3 %all-reduce.12.cloned.1.call-start = ((), (), s32[]{:S(2)}) async-start(), calls=%async_computation.22 | async-start | bytes 8912896 | tf_op jit(solution)/shard_map/psum | solution.py:133
  946.3 174.5 %copy-start.15 = (f32[8,1,512]{2,1,0:T(1,128)S(1)}, f32[8,1,512]{2,1,0:T(1,128)}, u32[]{:S(2)}) copy-start(f32[8,1,512]{2,1,0:T(1,128)} %copy-done.14) | copy-start | bytes 49156
  946.3 174.5 %copy-start.28 = (f32[256]{0:T(256)S(1)}, f32[256]{0:T(256)}, u32[]{:S(2)}) copy-start(f32[256]{0:T(256)} %copy-done.27) | copy-start | bytes 3076
  951.6 275.6 %reduce-scatter.12.cloned.1.call-start = ((), (), s32[]{:S(2)}) async-start(), calls=%async_computation.17 | async-start | bytes 4718592 | tf_op jit(solution)/shard_map/reduce_scatter | solution.py:214
  1119.0 1.1 copy-start.16
  1120.1 0.6 copy-start.18
  1124.2 1.0 copy-start.9
  1124.3 125.4 %reduce-scatter.14.cloned.1.call-start = ((), (), s32[]{:S(2)}) async-start(), calls=%async_computation.18 | async-start | bytes 9437184 | tf_op jit(solution)/shard_map/reduce_scatter | solution.py:211
  1133.6 191.0 %reduce-scatter.10.cloned.1.call-start = ((), (), s32[]{:S(2)}) async-start(), calls=%async_computation.16 | async-start | bytes 9437184 | tf_op jit(solution)/shard_map/reduce_scatter | solution.py:208
  1139.5 344.7 %reduce-scatter.20.cloned.1.call-start = ((), (), s32[]{:S(2)}) async-start(), calls=%async_computation.21 | async-start | bytes 28311552 | tf_op jit(solution)/shard_map/reduce_scatter | solution.py:156
  1153.7 490.3 %reduce-scatter.18.cloned.1.call-start = ((), (), s32[]{:S(2)}) async-start(), calls=%async_computation.20 | async-start | bytes 28311552 | tf_op jit(solution)/shard_map/reduce_scatter | solution.py:153
  1167.6 636.2 %reduce-scatter.16.cloned.1.call-start = ((), (), s32[]{:S(2)}) async-start(), calls=%async_computation.19 | async-start | bytes 28311552 | tf_op jit(solution)/shard_map/reduce_scatter | solution.py:150
  1181.1 0.7 copy-start.30
  1181.1 1.9 copy-start.17
  1181.1 1.9 copy-start.19
  1183.0 7.2 copy-start.22
Sparse Core Ops, SparseCore 0:
  9.9 39.4 all-gather.8
  51.2 54.7 all-gather.10
  107.9 55.8 all-gather.12
  171.9 154.9 all-reduce.7
  328.7 124.1 all-gather.16
  454.6 125.1 all-gather.14
  581.7 130.1 all-gather.18
  757.6 154.9 all-reduce.9
  938.0 13.5 reduce-scatter.7
  954.6 163.4 all-reduce.11
  1124.4 50.1 reduce-scatter.11
  1177.9 71.7 reduce-scatter.13
  1253.1 71.4 reduce-scatter.9
  1328.1 156.0 reduce-scatter.19
  1487.6 156.2 reduce-scatter.17
  1647.4 156.2 reduce-scatter.15
where the time goes:
time: 1820 us
  waiting for transfers between devices  1460 us (80%)
  matrix products  191 us (10%)
  blocking collectives  70.5 us (4%)
  other arithmetic  57.7 us (3%)
    psum x1, waiting for transfers between devices, shards(): lax.psum(matmul(hidden, full_down).astype(jnp.bfloat16), 'tensor')  166 us
    reduce_scatter x1, waiting for transfers between devices, shards(): lax.psum_scatter(grad_down.astype(jnp.bfloat16), ('dp', 'seq'), scatter_d...  157 us
    reduce_scatter x1, waiting for transfers between devices, shards(): lax.psum_scatter(grad_gate.astype(jnp.bfloat16), ('dp', 'seq'), scatter_d...  154 us
    reduce_scatter x1, waiting for transfers between devices, shards(): lax.psum_scatter(grad_up.astype(jnp.bfloat16), ('dp', 'seq'), scatter_dim...  154 us
    psum x1, waiting for transfers between devices, shards(): lax.psum(matmul_nt(d_gate, back_gate) + matmul_nt(d_up, back_up), 'tensor')  140 us
    psum x1, waiting for transfers between devices, shards(): attn = lax.psum(matmul(mixed, full_out), 'tensor')  136 us
    all_gather x1, waiting for transfers between devices, shards(): lax.all_gather(w_up, ('dp', 'seq'), axis=0, tiled=True)  119 us
    all_gather x1, waiting for transfers between devices, shards(): lax.all_gather(w_down, ('dp', 'seq'), axis=1, tiled=True)  118 us
  transfers between devices with their start and end apart: 16, of which 15 were waited for; matrix products, arithmetic and copies ran while one was open for 9% of the time, Pallas kernels for 0%

commit v1 on v0

--- a/solution.py
+++ b/solution.py
@@ -130,7 +130,9 @@
     up_val = matmul(act_two, full_up)
     gelu_val, gelu_pull = jax.vjp(gelu_tanh, gate)
     hidden = (gelu_val * up_val).astype(jnp.bfloat16)
-    ffn = lax.psum(matmul(hidden, full_down).astype(jnp.bfloat16), "tensor").astype(jnp.float32)
+    ffn = jnp.sum(
+        lax.all_gather(matmul(hidden, full_down).astype(jnp.bfloat16), "tensor"), axis=0
+    ).astype(jnp.float32)
     out = (resid + ffn).astype(jnp.bfloat16)
     back_gate, back_up, back_down = (
         lax.all_gather(w_gate, ("dp", "seq"), axis=0, tiled=True),

time: 1820 us -> 1910 us (1.049)
  waiting for transfers between devices: 1460 us -> 1540 us
    all_gather x0 -> x1, waiting for transfers between devices: none -> 145 us  [shards(): lax.all_gather(matmul(hidden, full_down).astype(jnp.bfloat16), 'tensor')]
    psum x1, waiting for transfers between devices: 166 us -> 97.6 us  [shards(): lax.psum(d_act_query.astype(jnp.bfloat16), 'tensor').astype(jnp.float32)]
  transfers between devices with their start and end apart: 16 -> 17, of which waited for: 15 -> 16; matrix products, arithmetic and copies ran while one was open for 9% -> 9% of each run, Pallas kernels for 0% -> 0%
where the time goes in v1:
time: 1910 us; the launch traced here: 1900 us
  waiting for transfers between devices  1540 us (81%)
  matrix products  192 us (10%)
  blocking collectives  70.3 us (4%)
  other arithmetic  66.9 us (4%)
    reduce_scatter x1, waiting for transfers between devices, shards(): lax.psum_scatter(grad_down.astype(jnp.bfloat16), ('dp', 'seq'), scatter_d...  157 us
    reduce_scatter x1, waiting for transfers between devices, shards(): lax.psum_scatter(grad_gate.astype(jnp.bfloat16), ('dp', 'seq'), scatter_d...  154 us
    reduce_scatter x1, waiting for transfers between devices, shards(): lax.psum_scatter(grad_up.astype(jnp.bfloat16), ('dp', 'seq'), scatter_dim...  154 us
    all_gather x1, waiting for transfers between devices, shards(): lax.all_gather(matmul(hidden, full_down).astype(jnp.bfloat16), 'tensor')  145 us
    psum x1, waiting for transfers between devices, shards(): lax.psum(matmul_nt(d_gate, back_gate) + matmul_nt(d_up, back_up), 'tensor')  140 us
    psum x1, waiting for transfers between devices, shards(): attn = lax.psum(matmul(mixed, full_out), 'tensor')  136 us
    all_gather x1, waiting for transfers between devices, shards(): lax.all_gather(w_up, ('dp', 'seq'), axis=0, tiled=True)  119 us
    all_gather x1, waiting for transfers between devices, shards(): lax.all_gather(w_down, ('dp', 'seq'), axis=1, tiled=True)  118 us
  transfers between devices with their start and end apart: 17, of which 16 were waited for; matrix products, arithmetic and copies ran while one was open for 9% of the time, Pallas kernels for 0%

profile of v1, /device:TPU:0, one launch (start us, length us, event | category | flops | bytes accessed | tf_op | source)
XLA Modules:
  0.0 1903.1 jit_solution(14445449040157003903)
XLA Ops:
  12.5 18.0 all-gather.1
  31.4 17.9 all-gather.11.cloned.1.call-done
  49.4 3.5 fusion.48
  53.7 10.2 all_gather.41
  63.8 42.2 %all-gather.13.cloned.1.call-done = bf16[4096,1024]{1,0:T(8,128)(2,1)} async-done(((bf16[512,1024]{1,0:T(8,128)(2,1)}), bf16[4096,1024]{1,0:T(8,128)(2,1)}) %all-gather.13.cloned.1.call-update) | async-done | bytes 8388624 | tf_op jit(solution)/shard_map/all_gather | solution.py:82
  106.0 6.8 fusion.46
  113.0 1.0 pad_maximum_fusion
  114.1 1.7 copy.57
  115.8 1.5 fusion.23
  117.7 0.9 copy-done.3
  119.2 1.5 convolution_convert_fusion.9
  120.7 43.1 %all-gather.15.cloned.1.call-done = bf16[1024,4096]{1,0:T(8,128)(2,1)} async-done(((bf16[1024,512]{1,0:T(8,128)(2,1)}), bf16[1024,4096]{1,0:T(8,128)(2,1)}) %all-gather.15.cloned.1.call-update) | async-done | bytes 8388624 | tf_op jit(solution)/shard_map/all_gather | solution.py:83
  163.8 8.0 fusion.51
  174.5 16.3 all-gather.2
  191.4 135.5 %all-reduce.8.cloned.1.call-done = f32[256,4096]{1,0:T(8,128)} async-done(((f32[256,4096]{1,0:T(8,128)}), f32[256,4096]{1,0:T(8,128)}) %all-reduce.8.cloned.1.call-update) | async-done | bytes 4194320 | tf_op jit(solution)/shard_map/psum | solution.py:117
  326.9 2.8 multiply_reduce_fusion.2
  329.8 2.0 copy-done
  331.8 1.9 multiply_convert_fusion
  333.7 119.2 %all-gather.19.cloned.1.call-done = bf16[4096,3072]{1,0:T(8,128)(2,1)} async-done(((bf16[512,3072]{1,0:T(8,128)(2,1)}), bf16[4096,3072]{1,0:T(8,128)(2,1)}) %all-gather.19.cloned.1.call-update) | async-done | bytes 25165840 | tf_op jit(solution)/shard_map/all_gather | solution.py:121
  452.9 13.7 fusion.53
  466.6 113.3 %all-gather.17.cloned.1.call-done = bf16[4096,3072]{1,0:T(8,128)(2,1)} async-done(((bf16[512,3072]{1,0:T(8,128)(2,1)}), bf16[4096,3072]{1,0:T(8,128)(2,1)}) %all-gather.17.cloned.1.call-update) | async-done | bytes 25165840 | tf_op jit(solution)/shard_map/all_gather | solution.py:120
  579.8 13.6 fusion.52
  593.4 118.5 %all-gather.21.cloned.1.call-done = bf16[3072,4096]{1,0:T(8,128)(2,1)} async-done(((bf16[3072,512]{1,0:T(8,128)(2,1)}), bf16[3072,4096]{1,0:T(8,128)(2,1)}) %all-gather.21.cloned.1.call-update) | async-done | bytes 25165840 | tf_op jit(solution)/shard_map/all_gather | solution.py:122
  711.9 17.4 multiply_convert_fusion.1
  729.3 13.4 fusion.54
  742.7 15.0 convolution_add_fusion.1
  757.7 13.8 convolution_convert_fusion.7
  771.6 1.3 log_add_fusion
  772.9 139.9 %all-reduce.10.cloned.1.call-done = f32[256,4096]{1,0:T(8,128)} async-done(((f32[256,4096]{1,0:T(8,128)}), f32[256,4096]{1,0:T(8,128)}) %all-reduce.10.cloned.1.call-update) | async-done | bytes 4194320 | tf_op jit(solution)/shard_map/psum | solution.py:148
  912.8 5.3 multiply_reduce_fusion
  918.7 144.9 %all-gather.23.cloned.1.call-done = bf16[1024,4096]{1,0:T(8,128)(2,1)} async-done(((bf16[256,4096]{1,0:T(8,128)(2,1)}), bf16[1024,4096]{1,0:T(8,128)(2,1)}) %all-gather.23.cloned.1.call-update) | async-done | bytes 8388624 | tf_op jit(solution)/shard_map/all_gather | solution.py:134
  1063.6 6.9 reduce_sum.87
  1070.5 7.8 multiply_add_fusion
  1078.3 2.0 copy-done.2
  1080.3 6.6 convolution_convert_fusion.8
  1086.9 2.0 copy.83
  1088.9 2.3 fusion.28
  1094.8 1.0 add_convert_fusion.1
  1095.9 7.3 convolution_convert_fusion.6
  1103.1 4.4 reduce-scatter.8.cloned.1.call-done
  1107.6 97.6 %all-reduce.12.cloned.1.call-done = (bf16[256,4096]{1,0:T(8,128)(2,1)}, bf16[256,512]{1,0:T(8,128)(2,1)}) async-done(((bf16[256,4096]{1,0:T(8,128)(2,1)}, bf16[256,512]{1,0:T(8,128)(2,1)}), (bf16[256,4096]{1,0:T(8,128)(2,1)}, bf16[256,512]{1,0:T(8,128)(2,1)})) %all-reduce.12.cloned.1.call-update) | async-done | bytes 2359312 | tf_op jit(solution)/shard_map/psum | solution.py:198
  1205.2 0.9 slice.84
  1206.1 1.0 convert_element_type.161
  1207.9 3.5 convolution_convert_fusion.5
  1211.4 1.0 copy-done.7
  1212.4 8.3 convolution_convert_fusion.3
  1221.4 5.8 convolution_convert_fusion.4
  1227.5 13.7 convolution_convert_fusion
  1241.2 13.9 convolution_convert_fusion.1
  1255.2 13.5 convolution_convert_fusion.2
  1270.6 7.2 fusion.9
  1277.8 25.8 %all-reduce.2 = (bf16[4096]{0:T(1024)(128)(2,1)S(1)}, bf16[4096]{0:T(1024)(128)(2,1)S(1)}) all-reduce(bf16[4096]{0:T(1024)(128)(2,1)S(1)} %get-tuple-element.12, bf16[4096]{0:T(1024)(128)(2,1)S(1)} %copy-done.19), channel_id=4, replica_groups=mesh['dp'=4,'seq'=2,'tensor'=4] {'dp','seq'}, use_global_device_ids=true, to_apply=%region_16.17.clone | all-reduce | flops 8192 | bytes 32768
  1304.2 7.2 fusion.8
  1311.5 2.2 convert_element_type.167
  1313.6 23.4 %reduce-scatter.14.cloned.1.call-done = bf16[1024,512]{1,0:T(8,128)(2,1)} async-done(((bf16[1024,4096]{1,0:T(8,128)(2,1)}), bf16[1024,512]{1,0:T(8,128)(2,1)}) %reduce-scatter.14.cloned.1.call-update) | async-done | bytes 1048592 | tf_op jit(solution)/shard_map/reduce_scatter | solution.py:213
  1337.0 2.8 convert_element_type.169
  1339.8 72.0 %reduce-scatter.10.cloned.1.call-done = bf16[512,1024]{1,0:T(8,128)(2,1)} async-done(((bf16[4096,1024]{1,0:T(8,128)(2,1)}), bf16[512,1024]{1,0:T(8,128)(2,1)}) %reduce-scatter.10.cloned.1.call-update) | async-done | bytes 1048592 | tf_op jit(solution)/shard_map/reduce_scatter | solution.py:210
  1411.9 2.8 convert_element_type.165
  1414.6 156.7 %reduce-scatter.20.cloned.1.call-done = bf16[3072,512]{1,0:T(8,128)(2,1)} async-done(((bf16[3072,4096]{1,0:T(8,128)(2,1)}), bf16[3072,512]{1,0:T(8,128)(2,1)}) %reduce-scatter.20.cloned.1.call-update) | async-done | bytes 3145744 | tf_op jit(solution)/shard_map/reduce_scatter | solution.py:158
  1571.3 5.5 convert_element_type.177
  1576.8 154.3 %reduce-scatter.18.cloned.1.call-done = bf16[512,3072]{1,0:T(8,128)(2,1)} async-done(((bf16[4096,3072]{1,0:T(8,128)(2,1)}), bf16[512,3072]{1,0:T(8,128)(2,1)}) %reduce-scatter.18.cloned.1.call-update) | async-done | bytes 3145744 | tf_op jit(solution)/shard_map/reduce_scatter | solution.py:155
  1731.1 5.4 convert_element_type.175
  1736.5 154.4 %reduce-scatter.16.cloned.1.call-done = bf16[512,3072]{1,0:T(8,128)(2,1)} async-done(((bf16[4096,3072]{1,0:T(8,128)(2,1)}), bf16[512,3072]{1,0:T(8,128)(2,1)}) %reduce-scatter.16.cloned.1.call-update) | async-done | bytes 3145744 | tf_op jit(solution)/shard_map/reduce_scatter | solution.py:152
  1890.9 5.4 convert_element_type.173
  (123 shorter events, 19.2 us)
Async XLA Ops:
  7.2 23.9 %copy-start.20 = (s32[512]{0:T(512)S(1)}, s32[512]{0:T(512)}, u32[]{:S(2)}) copy-start(s32[512]{0:T(512)} %param.12) | copy-start | bytes 6148
  7.2 23.4 %copy-start.1 = (bf16[256,4096]{1,0:T(8,128)(2,1)S(1)}, bf16[256,4096]{1,0:T(8,128)(2,1)}, u32[]{:S(2)}) copy-start(bf16[256,4096]{1,0:T(8,128)(2,1)} %param.11) | copy-start | bytes 6291460
  7.2 42.2 %all-gather.11.cloned.1.call-start = ((), (), s32[]{:S(2)}) async-start(), calls=%async_computation.7 | async-start | bytes 4718592 | tf_op jit(solution)/shard_map/all_gather | solution.py:84
  7.9 98.1 %all-gather.13.cloned.1.call-start = ((), (), s32[]{:S(2)}) async-start(), calls=%async_computation.8 | async-start | bytes 9437184 | tf_op jit(solution)/shard_map/all_gather | solution.py:82
  8.7 155.1 %all-gather.15.cloned.1.call-start = ((), (), s32[]{:S(2)}) async-start(), calls=%async_computation.9 | async-start | bytes 9437184 | tf_op jit(solution)/shard_map/all_gather | solution.py:83
  9.4 317.5 %all-reduce.8.cloned.1.call-start = ((), (), s32[]{:S(2)}) async-start(), calls=%async_computation.10 | async-start | bytes 8388608 | tf_op jit(solution)/shard_map/psum | solution.py:117
  31.1 21.7 %copy-start.21 = (f32[256]{0:T(256)}, f32[256]{0:T(256)S(1)}, u32[]{:S(2)}) copy-start(f32[256]{0:T(256)S(1)} %add_rsqrt_fusion.1) | copy-start | bytes 3076
  53.5 59.4 %copy-start.9 = (f32[256,128]{0,1:T(8,128)}, f32[256,128]{0,1:T(8,128)S(1)}, u32[]{:S(2)}) copy-start(f32[256,128]{0,1:T(8,128)S(1)} %copy.54) | copy-start | bytes 393220
  53.6 59.3 %copy-start.11 = (f32[256,128]{0,1:T(8,128)}, f32[256,128]{0,1:T(8,128)S(1)}, u32[]{:S(2)}) copy-start(f32[256,128]{0,1:T(8,128)S(1)} %copy.56) | copy-start | bytes 393220
  115.7 3.5 copy-start.5
  117.3 1.3 copy-start.3
  117.3 1.3 copy-start.17
  118.6 0.6 copy-start.24
  171.8 281.1 %all-gather.19.cloned.1.call-start = ((), (), s32[]{:S(2)}) async-start(), calls=%async_computation.12 | async-start | bytes 28311552 | tf_op jit(solution)/shard_map/all_gather | solution.py:121
  172.4 407.4 %all-gather.17.cloned.1.call-start = ((), (), s32[]{:S(2)}) async-start(), calls=%async_computation.11 | async-start | bytes 28311552 | tf_op jit(solution)/shard_map/all_gather | solution.py:120
  173.0 538.9 %all-gather.21.cloned.1.call-start = ((), (), s32[]{:S(2)}) async-start(), calls=%async_computation.13 | async-start | bytes 28311552 | tf_op jit(solution)/shard_map/all_gather | solution.py:122
  173.7 739.1 %all-reduce.10.cloned.1.call-start = ((), (), s32[]{:S(2)}) async-start(), calls=%async_computation.14 | async-start | bytes 8388608 | tf_op jit(solution)/shard_map/psum | solution.py:148
  326.9 4.9 copy-start.12
  329.8 2.0 copy-start
  329.8 2.0 copy-start.25
  757.7 305.9 %all-gather.23.cloned.1.call-start = ((), (), s32[]{:S(2)}) async-start(), calls=%async_computation.22 | async-start | bytes 10485760 | tf_op jit(solution)/shard_map/all_gather | solution.py:134
  771.6 336.0 %reduce-scatter.8.cloned.1.call-start = ((), (), s32[]{:S(2)}) async-start(), calls=%async_computation.15 | async-start | bytes 786432 | tf_op jit(solution)/shard_map/reduce_scatter | solution.py:190
  1078.3 2.0 copy-start.2
  1088.9 2.4 copy-start.4
  1088.9 2.5 copy-start.6
  1088.9 2.6 copy-start.8
  1088.9 2.6 copy-start.18
  1092.8 2.0 copy-start.10
  1094.6 110.7 %all-reduce.12.cloned.1.call-start = ((), (), s32[]{:S(2)}) async-start(), calls=%async_computation.23 | async-start | bytes 4718592 | tf_op jit(solution)/shard_map/psum | solution.py:198
  1103.1 104.7 %copy-start.22 = (f32[256]{0:T(256)S(1)}, f32[256]{0:T(256)}, u32[]{:S(2)}) copy-start(f32[256]{0:T(256)} %copy-done.21) | copy-start | bytes 3076
  1107.6 203.9 %reduce-scatter.12.cloned.1.call-start = ((), (), s32[]{:S(2)}) async-start(), calls=%async_computation.17 | async-start | bytes 4718592 | tf_op jit(solution)/shard_map/reduce_scatter | solution.py:216
  1207.2 0.6 copy-start.13
  1207.2 0.6 copy-start.15
  1211.3 1.0 copy-start.7
  1211.3 125.6 %reduce-scatter.14.cloned.1.call-start = ((), (), s32[]{:S(2)}) async-start(), calls=%async_computation.18 | async-start | bytes 9437184 | tf_op jit(solution)/shard_map/reduce_scatter | solution.py:213
  1220.7 0.7 copy-start.23
  1220.7 191.2 %reduce-scatter.10.cloned.1.call-start = ((), (), s32[]{:S(2)}) async-start(), calls=%async_computation.16 | async-start | bytes 9437184 | tf_op jit(solution)/shard_map/reduce_scatter | solution.py:210
  1227.2 344.1 %reduce-scatter.20.cloned.1.call-start = ((), (), s32[]{:S(2)}) async-start(), calls=%async_computation.21 | async-start | bytes 28311552 | tf_op jit(solution)/shard_map/reduce_scatter | solution.py:158
  1241.2 490.0 %reduce-scatter.18.cloned.1.call-start = ((), (), s32[]{:S(2)}) async-start(), calls=%async_computation.20 | async-start | bytes 28311552 | tf_op jit(solution)/shard_map/reduce_scatter | solution.py:155
  1255.1 635.8 %reduce-scatter.16.cloned.1.call-start = ((), (), s32[]{:S(2)}) async-start(), calls=%async_computation.19 | async-start | bytes 28311552 | tf_op jit(solution)/shard_map/reduce_scatter | solution.py:152
  1268.6 0.7 copy-start.26
  1268.6 1.9 copy-start.14
  1268.7 1.9 copy-start.16
  1270.6 7.2 copy-start.19
Sparse Core Ops, SparseCore 0:
  9.9 39.4 all-gather.10
  51.2 54.7 all-gather.12
  107.9 55.8 all-gather.14
  171.9 154.9 all-reduce.7
  328.7 124.1 all-gather.18
  454.6 125.1 all-gather.16
  581.7 130.1 all-gather.20
  757.8 154.9 all-reduce.9
  915.0 148.5 all-gather.22
  1094.7 12.8 reduce-scatter.7
  1110.5 94.6 all-reduce.11
  1211.5 50.1 reduce-scatter.11
  1265.2 71.7 reduce-scatter.13
  1340.3 71.5 reduce-scatter.9
  1415.3 155.9 reduce-scatter.19
  1574.8 156.2 reduce-scatter.17
  1734.6 156.2 reduce-scatter.15
